TPU v7x, 256 devices: a whole 4x4x8 slice. The times are simulated.
256 devices in a mesh: unit: 4 (over y), bank: 4 (over x), zero: 16 (over z, core).
Axes of the slice: x: 4, y: 4, z: 8, core: 2. Of those that a mesh axis runs over, the one named last changes fastest.
Arguments:
- train_down: float32 [256, 1024, 2048], P(('unit', 'bank'), None, 'zero'), parts along dimension 0, may hold values from -0.25 to 0.25
- router_weight: float32 [8192, 64], P(('unit', 'zero'), 'bank'), parts along dimension 0, may hold values from -0.125 to 0.125
- router_gain: float32 [8192], P(('unit', 'zero')), parts along dimension 0, may hold values from 0.25 to 1.75
Outputs:
- ready_down: bfloat16 [256, 1024, 2048], P(('unit', 'bank'), 'zero'), parts along dimension 0
- scale_down: float32 [256, 1024], P(('unit', 'bank'), 'zero'), parts along dimension 0
- serve_router: bfloat16 [8192, 64], P('unit'), parts along dimension 0
There are 4 independent parts, one for each index of `unit`. A program takes and returns all parts, laid end to end along the dimension named above; each array names one. Nothing has to cross between parts.
All inputs are finite; a program needn't handle non-finite values.
Results may differ from a plain program's by a relative error of at most 0.001.
Values may be sent and summed in bfloat16 or wider, within the bound.
A program may use at most 128 MiB of HBM per device.

v0:
```python
import jax
import jax.numpy as jnp
from jax import lax
from jax.sharding import Mesh
from jax.sharding import PartitionSpec as P

ZERO = ("zero_0", "zero_1")
UNIT_ZERO = ("unit", "zero_0", "zero_1")


def gathered_total(value, axis):
    tiles = lax.all_gather(value, axis)
    return tiles.max(axis=0)


def in_blocks(value, dim, length):
    return jnp.stack(jnp.split(value, length, axis=dim))


def joined_along(tiles, dim):
    tiles = jnp.moveaxis(tiles, 0, dim)
    dims = tiles.shape
    return tiles.reshape(*dims[:dim], dims[dim] * dims[dim + 1], *dims[dim + 2 :])


def turned_blocks(tiles, axes, sequence):
    dims = [lax.axis_size(a) for a in axes]
    tiles = tiles.reshape(*dims, *tiles.shape[1:])
    for k in sequence:
        tiles = lax.all_to_all(tiles, axes[k], split_axis=k, concat_axis=k, tiled=True)
    return tiles.reshape(-1, *tiles.shape[len(axes) :])


def two_step_exchange(value, groups, sequence, split_dim, concat_dim):
    length = lax.axis_size(groups[0]) * lax.axis_size(groups[1])
    tiles = in_blocks(value, split_dim, length)
    return joined_along(turned_blocks(tiles, groups, sequence), concat_dim)


def per_device(train_down, router_weight, router_gain):
    scale_down = gathered_total(jnp.max(jnp.abs(train_down), axis=2), ZERO)
    narrow_down = (train_down / jnp.expand_dims(scale_down, 2)).astype(jnp.bfloat16)
    ready_down = two_step_exchange(narrow_down, ("zero_0", "zero_1"), (1, 0), 1, 2)
    scale_down = lax.dynamic_slice_in_dim(
        scale_down, lax.axis_index(ZERO) * ready_down.shape[1], ready_down.shape[1], axis=1
    )
    part_router = (router_weight * router_gain[:, None]).astype(jnp.bfloat16)
    row_router = lax.all_gather(part_router, ZERO, axis=0, tiled=True)
    serve_router = lax.all_gather(row_router, "bank", axis=1, tiled=True)
    return (ready_down, scale_down, serve_router)


def solution(mesh):
    torus = Mesh(
        mesh.devices.reshape(mesh.shape["unit"], mesh.shape["bank"], 8, 2),
        ("unit", "bank", "zero_0", "zero_1"),
    )
    placed = (P(("unit", "bank"), None, ZERO), P(UNIT_ZERO, "bank"), P(UNIT_ZERO))
    return jax.shard_map(
        per_device,
        mesh=torus,
        in_specs=placed,
        out_specs=(P(("unit", "bank"), ZERO, None), P(("unit", "bank"), ZERO), P("unit", None)),
        check_vma=False,
    )
```

profile of v0, /device:TPU:2, one launch (start us, length us, event | category | flops | bytes accessed | tf_op | source)
XLA Modules:
  0.0 208.9 jit_solution(14406718394577058157)
XLA Ops:
  7.2 0.0 all-gather.3.cloned.1.call-start
  7.2 6.2 %abs_reduce_fusion = f32[16,1024]{1,0:T(8,128)} fusion(f32[16,1024,128]{2,1,0:T(8,128)} %param.3), kind=kLoop, calls=%fused_computation.1 | loop fusion | flops 4177920 | bytes 8454144 | tf_op jit(solution)/shard_map/reduce_max | solution.py:41
  13.5 0.0 all-gather.3.cloned.1.call-update
  13.5 41.7 %all-gather.3.cloned.1.call-done = f32[256,1024]{1,0:T(8,128)} async-done(((f32[16,1024]{1,0:T(8,128)}), f32[256,1024]{1,0:T(8,128)}) %all-gather.3.cloned.1.call-update) | async-done | bytes 1048592 | tf_op jit(solution)/shard_map/all_gather | solution.py:12
  55.1 1.3 reduce_max.19
  56.4 5.3 %divide_convert_fusion = bf16[16,1024,128]{2,1,0:T(8,128)(2,1)S(1)} fusion(f32[16,1024,128]{2,1,0:T(8,128)} %param.3, f32[16,1024]{1,0:T(8,128)S(1)} %reduce_max.19), kind=kLoop, calls=%fused_computation | loop fusion | flops 4194304 | bytes 12648448 | tf_op jit(solution)/shard_map/convert_element_type | solution.py:42
  62.4 1.3 copy.12
  63.7 7.1 %all_to_all.10 = bf16[8,2,16,64,128]{4,3,2,0,1:T(8,128)(2,1)S(1)} all-to-all(bf16[8,2,16,64,128]{4,3,2,0,1:T(8,128)(2,1)S(1)} %copy.12), channel_id=1, replica_groups=mesh['unit'=4,'bank'=4,'zero_0'=8,'zero_1'=2] {'zero_1'}, dimensions={1} | all-to-all | bytes 8388608 | tf_op jit(solution)/shard_map/all_to_all | solution.py:30
  70.8 3.0 %copy.13 = bf16[8,2,16,64,128]{4,3,2,1,0:T(8,128)(2,1)} copy(bf16[8,2,16,64,128]{4,3,2,0,1:T(8,128)(2,1)S(1)} %all_to_all.10) | data formatting | bytes 8388608 | tf_op jit(solution)/shard_map/all_to_all | solution.py:30
  73.8 0.0 copy-start
  73.8 0.0 copy-start.1
  73.8 4.7 %all-to-all-start.1 = ((bf16[8,2,16,64,128]{4,3,2,1,0:T(8,128)(2,1)}), bf16[8,2,16,64,128]{4,3,2,1,0:T(8,128)(2,1)}, u32[]{:S(2)}, u32[]{:S(2)}) async-start(bf16[8,2,16,64,128]{4,3,2,1,0:T(8,128)(2,1)} %copy.13), calls=%async_computation.1 | async-start | bytes 8388608 | tf_op jit(solution)/shard_map/all_to_all | solution.py:30
  78.5 0.0 copy-done
  78.5 0.0 copy-done.1
  78.5 104.4 %all_gather.14 = bf16[2048,16]{0,1:T(8,128)(2,1)S(1)} all-gather(bf16[128,16]{0,1:T(8,128)(2,1)S(1)} %multiply_convert_fusion), channel_id=1, replica_groups=mesh['unit'=4,'bank'=4,'zero_0'=8,'zero_1'=2] {'zero_0','zero_1'}, dimensions={0}, use_global_device_ids=true | all-gather | bytes 69632 | tf_op jit(solution)/shard_map/all_gather | solution.py:48
  182.9 12.5 %all_gather.15 = bf16[2048,64]{0,1:T(8,128)(2,1)S(1)} all-gather(bf16[2048,16]{0,1:T(8,128)(2,1)S(1)} %all_gather.14), channel_id=1, replica_groups=mesh['unit'=4,'bank'=4,'zero_0'=8,'zero_1'=2] {'bank'}, dimensions={1}, use_global_device_ids=true | all-gather | bytes 327680 | tf_op jit(solution)/shard_map/all_gather | solution.py:49
  195.4 0.7 constant_dynamic-slice_fusion
  196.0 0.0 all-to-all-done.1
  196.0 5.3 %copy.17 = bf16[16,16,8,8,128]{4,3,0,2,1:T(8,128)(2,1)} copy(bf16[16,16,8,8,128]{4,3,2,1,0:T(8,128)(2,1)} %bitcast.21) | data formatting | bytes 8388608 | tf_op jit(solution)/shard_map/reshape | solution.py:23
  201.4 0.7 copy.34
  (17 shorter events, 0.6 us)
Async XLA Ops:
  7.2 48.0 %all-gather.3.cloned.1.call-start = ((), (), s32[]{:S(2)}) async-start(), calls=%async_computation.2 | async-start | bytes 1114112 | tf_op jit(solution)/shard_map/all_gather | solution.py:12
  73.8 4.7 %copy-start = (f32[128,16]{0,1:T(8,128)S(1)}, f32[128,16]{0,1:T(8,128)}, u32[]{:S(2)}) copy-start(f32[128,16]{0,1:T(8,128)} %param.4) | copy-start | bytes 24580
  73.8 4.7 %copy-start.1 = (f32[128]{0:T(128)S(1)}, f32[128]{0:T(128)}, u32[]{:S(2)}) copy-start(f32[128]{0:T(128)} %param.5) | copy-start | bytes 1540
  73.8 122.2 %all-to-all-start.1 = ((bf16[8,2,16,64,128]{4,3,2,1,0:T(8,128)(2,1)}), bf16[8,2,16,64,128]{4,3,2,1,0:T(8,128)(2,1)}, u32[]{:S(2)}, u32[]{:S(2)}) async-start(bf16[8,2,16,64,128]{4,3,2,1,0:T(8,128)(2,1)} %copy.13), calls=%async_computation.1 | async-start | bytes 8388608 | tf_op jit(solution)/shard_map/all_to_all | solution.py:30
Sparse Core Ops, SparseCore 0:
  13.6 41.4 all-gather.2
where the time goes:
time: 209 us
  blocking collectives  124 us (59%)
  waiting for transfers between devices  41.7 us (20%)
  between operations  14.2 us (7%)
  other arithmetic  12.8 us (6%)
  local copies, waits for them, and re-layouts  11.6 us (6%)
  starting transfers between devices  4.71 us (2%)
    all_gather x1, blocking collectives, per_device(): row_router = lax.all_gather(part_router, ZERO, axis=0, tiled=True)  104 us
    all_gather x1, waiting for transfers between devices, gathered_total(): tiles = lax.all_gather(value, axis)  41.7 us
    all_gather x1, blocking collectives, per_device(): serve_router = lax.all_gather(row_router, 'bank', axis=1, tiled=True)  12.5 us
    all_to_all x1, blocking collectives, turned_blocks(): lax.all_to_all(tiles, axes[k], split_axis=k, concat_axis=k, tiled=True)  7.1 us
    reduce_max x1, other arithmetic, per_device(): scale_down = gathered_total(jnp.max(jnp.abs(train_down), axis=2), ZERO)  6.25 us
    reshape x1, local copies, waits for them, and re-layouts, joined_along(): tiles.reshape(*dims[:dim], dims[dim] * dims[dim + 1], *dims[dim + 2:])  5.35 us
    convert_element_type x1, other arithmetic, per_device(): (train_down / jnp.expand_dims(scale_down, 2)).astype(jnp.bfloat16)  5.26 us
    all_to_all x1, starting transfers between devices, turned_blocks(): lax.all_to_all(tiles, axes[k], split_axis=k, concat_axis=k, tiled=True)  4.67 us
  transfers between devices with their start and end apart: 2, of which 1 were waited for; matrix products, arithmetic and copies ran while one was open for 0% of the time, Pallas kernels for 0%

commit v1 on v0

--- a/solution.py
+++ b/solution.py
@@ -46,7 +46,9 @@
     )
     part_router = (router_weight * router_gain[:, None]).astype(jnp.bfloat16)
     row_router = lax.all_gather(part_router, ZERO, axis=0, tiled=True)
-    serve_router = lax.all_gather(row_router, "bank", axis=1, tiled=True)
+    serve_router = jnp.concatenate(
+        lax.all_to_all(jnp.stack([row_router] * lax.axis_size("bank")), "bank", 0, 0), axis=1
+    )
     return (ready_down, scale_down, serve_router)
 
 

time: 209 us -> 198 us (0.947)
  blocking collectives: 124 us -> 28.3 us
  waiting for transfers between devices: 41.7 us -> 117 us
  starting transfers between devices: 4.71 us -> 9.39 us
  local copies, waits for them, and re-layouts: 11.6 us -> 14.8 us
    all_to_all x1, waiting for transfers between devices: 0.01 us -> 95.6 us  [turned_blocks(): lax.all_to_all(tiles, axes[k], split_axis=k, concat_axis=k, tiled=True)]
    all_gather x1, blocking collectives: 104 us -> 20.1 us  [per_device(): row_router = lax.all_gather(part_router, ZERO, axis=0, tiled=True)]
    all_gather x1, waiting for transfers between devices: 41.7 us -> 21.5 us  [gathered_total(): tiles = lax.all_gather(value, axis)]
    all_gather x1 -> x0, blocking collectives: 12.5 us -> none  [per_device(): serve_router = lax.all_gather(row_router, 'bank', axis=1, tiled=True)]
    all_to_all x0 -> x1, starting transfers between devices: none -> 4.8 us  [per_device(): lax.all_to_all(jnp.stack([row_router] * lax.axis_size('bank')), 'bank', 0...]
    all_to_all x1, local copies, waits for them, and re-layouts: 2.97 us -> 5.52 us  [turned_blocks(): lax.all_to_all(tiles, axes[k], split_axis=k, concat_axis=k, tiled=True)]
  transfers between devices with their start and end apart: 2 -> 3, of which waited for: 1 -> 2; matrix products, arithmetic and copies ran while one was open for 0% -> 3% of each run, Pallas kernels for 0% -> 0%
where the time goes in v1:
time: 198 us; the launch traced here: 197 us
  waiting for transfers between devices  117 us (59%)
  blocking collectives  28.3 us (14%)
  local copies, waits for them, and re-layouts  14.8 us (7%)
  between operations  14.2 us (7%)
  other arithmetic  12.8 us (6%)
  starting transfers between devices  9.39 us (5%)
    all_to_all x1, waiting for transfers between devices, turned_blocks(): lax.all_to_all(tiles, axes[k], split_axis=k, concat_axis=k, tiled=True)  95.6 us
    all_gather x1, waiting for transfers between devices, gathered_total(): tiles = lax.all_gather(value, axis)  21.5 us
    all_gather x1, blocking collectives, per_device(): row_router = lax.all_gather(part_router, ZERO, axis=0, tiled=True)  20.1 us
    all_to_all x1, blocking collectives, turned_blocks(): lax.all_to_all(tiles, axes[k], split_axis=k, concat_axis=k, tiled=True)  8.15 us
    reduce_max x1, other arithmetic, per_device(): scale_down = gathered_total(jnp.max(jnp.abs(train_down), axis=2), ZERO)  6.25 us
    all_to_all x1, local copies, waits for them, and re-layouts, turned_blocks(): lax.all_to_all(tiles, axes[k], split_axis=k, concat_axis=k, tiled=True)  5.52 us
    reshape x1, local copies, waits for them, and re-layouts, joined_along(): tiles.reshape(*dims[:dim], dims[dim] * dims[dim + 1], *dims[dim + 2:])  5.35 us
    convert_element_type x1, other arithmetic, per_device(): (train_down / jnp.expand_dims(scale_down, 2)).astype(jnp.bfloat16)  5.26 us
  transfers between devices with their start and end apart: 3, of which 2 were waited for; matrix products, arithmetic and copies ran while one was open for 3% of the time, Pallas kernels for 0%

profile of v1, /device:TPU:2, one launch (start us, length us, event | category | flops | bytes accessed | tf_op | source)
XLA Modules:
  0.0 196.6 jit_solution(3755257042915347789)
XLA Ops:
  7.2 0.0 copy-start
  7.2 0.0 copy-start.1
  7.2 0.0 all-gather.3.cloned.1.call-start
  7.2 6.2 %abs_reduce_fusion = f32[16,1024]{1,0:T(8,128)} fusion(f32[16,1024,128]{2,1,0:T(8,128)} %param.3), kind=kLoop, calls=%fused_computation.1 | loop fusion | flops 4177920 | bytes 8454144 | tf_op jit(solution)/shard_map/reduce_max | solution.py:41
  13.5 0.0 all-gather.3.cloned.1.call-update
  13.5 0.0 copy-done
  13.5 0.0 copy-done.1
  13.5 20.1 %all_gather.11 = bf16[2048,16]{0,1:T(8,128)(2,1)S(1)} all-gather(bf16[128,16]{0,1:T(8,128)(2,1)S(1)} %multiply_convert_fusion), channel_id=1, replica_groups=mesh['unit'=4,'bank'=4,'zero_0'=8,'zero_1'=2] {'zero_0','zero_1'}, dimensions={0}, use_global_device_ids=true | all-gather | bytes 69632 | tf_op jit(solution)/shard_map/all_gather | solution.py:48
  33.7 21.5 %all-gather.3.cloned.1.call-done = f32[256,1024]{1,0:T(8,128)} async-done(((f32[16,1024]{1,0:T(8,128)}), f32[256,1024]{1,0:T(8,128)}) %all-gather.3.cloned.1.call-update) | async-done | bytes 1048592 | tf_op jit(solution)/shard_map/all_gather | solution.py:12
  55.2 1.3 reduce_max.19
  56.5 5.3 %divide_convert_fusion = bf16[16,1024,128]{2,1,0:T(8,128)(2,1)S(1)} fusion(f32[16,1024,128]{2,1,0:T(8,128)} %param.3, f32[16,1024]{1,0:T(8,128)S(1)} %reduce_max.19), kind=kLoop, calls=%fused_computation | loop fusion | flops 4194304 | bytes 12648448 | tf_op jit(solution)/shard_map/convert_element_type | solution.py:42
  62.4 1.3 copy.12
  63.7 8.2 %all_to_all.15 = bf16[8,2,16,64,128]{4,3,2,0,1:T(8,128)(2,1)} all-to-all(bf16[8,2,16,64,128]{4,3,2,0,1:T(8,128)(2,1)S(1)} %copy.12), channel_id=1, replica_groups=mesh['unit'=4,'bank'=4,'zero_0'=8,'zero_1'=2] {'zero_1'}, dimensions={1} | all-to-all | bytes 8388608 | tf_op jit(solution)/shard_map/all_to_all | solution.py:30
  71.9 0.7 stack.75
  72.6 4.8 %all-to-all-start.2 = ((bf16[4,2048,16]{1,2,0:T(8,128)(2,1)}), bf16[4,2048,16]{1,2,0:T(8,128)(2,1)S(1)}, u32[]{:S(2)}, u32[]{:S(2)}) async-start(bf16[4,2048,16]{1,2,0:T(8,128)(2,1)} %stack.75), calls=%async_computation.2 | async-start | bytes 524288 | tf_op jit(solution)/shard_map/all_to_all | solution.py:50
  77.4 5.5 %copy.13 = bf16[8,2,16,64,128]{4,3,2,1,0:T(8,128)(2,1)} copy(bf16[8,2,16,64,128]{4,3,2,0,1:T(8,128)(2,1)} %all_to_all.15) | data formatting | bytes 8388608 | tf_op jit(solution)/shard_map/all_to_all | solution.py:30
  82.9 0.0 all-to-all-done.2
  82.9 4.5 %all-to-all-start.1 = ((bf16[8,2,16,64,128]{4,3,2,1,0:T(8,128)(2,1)}), bf16[8,2,16,64,128]{4,3,2,1,0:T(8,128)(2,1)}, u32[]{:S(2)}, u32[]{:S(2)}) async-start(bf16[8,2,16,64,128]{4,3,2,1,0:T(8,128)(2,1)} %copy.13), calls=%async_computation.1 | async-start | bytes 8388608 | tf_op jit(solution)/shard_map/all_to_all | solution.py:30
  87.5 0.7 constant_dynamic-slice_fusion
  88.2 95.6 %all-to-all-done.1 = bf16[8,2,16,64,128]{4,3,2,1,0:T(8,128)(2,1)} async-done(((bf16[8,2,16,64,128]{4,3,2,1,0:T(8,128)(2,1)}), bf16[8,2,16,64,128]{4,3,2,1,0:T(8,128)(2,1)}, u32[]{:S(2)}, u32[]{:S(2)}) %all-to-all-start.1) | async-done | bytes 4194336 | tf_op jit(solution)/shard_map/all_to_all | solution.py:30
  183.7 5.3 %copy.17 = bf16[16,16,8,8,128]{4,3,0,2,1:T(8,128)(2,1)} copy(bf16[16,16,8,8,128]{4,3,2,1,0:T(8,128)(2,1)} %bitcast.24) | data formatting | bytes 8388608 | tf_op jit(solution)/shard_map/reshape | solution.py:23
  189.1 0.7 copy.34
  (17 shorter events, 0.6 us)
Async XLA Ops:
  7.2 6.3 %copy-start = (f32[128,16]{0,1:T(8,128)S(1)}, f32[128,16]{0,1:T(8,128)}, u32[]{:S(2)}) copy-start(f32[128,16]{0,1:T(8,128)} %param.4) | copy-start | bytes 24580
  7.2 6.3 %copy-start.1 = (f32[128]{0:T(128)S(1)}, f32[128]{0:T(128)}, u32[]{:S(2)}) copy-start(f32[128]{0:T(128)} %param.5) | copy-start | bytes 1540
  7.2 48.0 %all-gather.3.cloned.1.call-start = ((), (), s32[]{:S(2)}) async-start(), calls=%async_computation.3 | async-start | bytes 1114112 | tf_op jit(solution)/shard_map/all_gather | solution.py:12
  72.6 10.3 %all-to-all-start.2 = ((bf16[4,2048,16]{1,2,0:T(8,128)(2,1)}), bf16[4,2048,16]{1,2,0:T(8,128)(2,1)S(1)}, u32[]{:S(2)}, u32[]{:S(2)}) async-start(bf16[4,2048,16]{1,2,0:T(8,128)(2,1)} %stack.75), calls=%async_computation.2 | async-start | bytes 524288 | tf_op jit(solution)/shard_map/all_to_all | solution.py:50
  82.9 100.8 %all-to-all-start.1 = ((bf16[8,2,16,64,128]{4,3,2,1,0:T(8,128)(2,1)}), bf16[8,2,16,64,128]{4,3,2,1,0:T(8,128)(2,1)}, u32[]{:S(2)}, u32[]{:S(2)}) async-start(bf16[8,2,16,64,128]{4,3,2,1,0:T(8,128)(2,1)} %copy.13), calls=%async_computation.1 | async-start | bytes 8388608 | tf_op jit(solution)/shard_map/all_to_all | solution.py:30
Sparse Core Ops, SparseCore 0:
  13.6 41.4 all-gather.2
